TPU v7x, 512 devices: a whole 4x8x8 slice. The times are simulated.
512 devices in a mesh: row: 32 (over y, x), col: 16 (over z, core).
Axes of the slice: x: 4, y: 8, z: 8, core: 2. Of those that a mesh axis runs over, the one named last changes fastest.
Arguments:
- tokens: bfloat16 [24576, 2048], P('row', 'col'), may hold values from -6 to 6
- out_grad: bfloat16 [24576, 2048], P('row', 'col'), may hold values from -3072 to 3072
- counts: int32 [32], P('row'), may hold values from 65 to 768
- block_moves: int32 [16, 3], replicated, may hold values from 0 to 31, as said below
- segment_ids: int32 [24576], P('row'), may hold values from 0 to 767, never falling along the last dimension, each value on 1 to 128 neighbouring positions
- gate_weight: bfloat16 [2048, 8192], P('row', 'col'), may hold values from -0.125 to 0.125
- up_weight: bfloat16 [2048, 8192], P('row', 'col'), may hold values from -0.125 to 0.125
- down_weight: bfloat16 [2048, 8192], P('row', 'col'), may hold values from -0.0625 to 0.0625
Outputs:
- hidden: bfloat16 [16384, 8192], P('row', 'col')
- gate_grad: float32 [2048, 8192], P('row', 'col')
- up_grad: float32 [2048, 8192], P('row', 'col')
- down_grad: float32 [2048, 8192], P('row', 'col')
Inputs may be any that keep to these rules, and one draw needn't show every extreme that they name: `block_moves`: each row is (source rank, destination rank, block index); the block is a valid block of its source; no two rows share both source and destination, nor both source and block; a rank is the source of at most two rows or the destination of at most one, never both; after the moves every rank holds at most 4 valid blocks and some hold exactly 4. `segment_ids`: never falling along the whole array; each document covers 1 to 128 consecutive slots.
All inputs are finite; a program needn't handle non-finite values.
Results may differ from a plain program's by a relative error of at most 0.015.
Values may be sent and summed in bfloat16 or wider, within the bound.
No kernel may reach another device: no remote copies, remote signals or barrier semaphores. Data moves between devices by JAX's collectives and lax.ppermute only.
A program may use at most 64 MiB of HBM per device.

v0:
```python
import jax
import jax.numpy as jnp
from jax import lax
from jax.sharding import Mesh
from jax.sharding import PartitionSpec as P

BLOCK = 128
WORK = 4
ROW = ("row_0", "row_1")


def side_by_side(arrays, axis, dim, along):
    both = jnp.concatenate(arrays, axis=along)
    filled, at, outs = (lax.all_gather(both, axis, axis=dim, tiled=True), 0, [])
    for a in arrays:
        outs.append(lax.slice_in_dim(filled, at, at + a.shape[along], axis=along))
        at += a.shape[along]
    return tuple(outs)


def own_rows(terms, axes):
    running = terms.astype(jnp.bfloat16)
    for axis in axes:
        running = lax.psum_scatter(running, axis, scatter_dimension=0, tiled=True)
    return running.astype(jnp.float32)


def local_terms(gate_sum, up_sum, back_sum):
    logistic = jax.nn.sigmoid(gate_sum)
    activated = gate_sum * logistic
    hidden = (activated * up_sum).astype(jnp.bfloat16)
    gate_back = (back_sum * up_sum * logistic * (1.0 + gate_sum * (1.0 - logistic))).astype(
        jnp.bfloat16
    )
    up_back = (back_sum * activated).astype(jnp.bfloat16)
    return (hidden, gate_back, up_back)


def contract(left_side, right_side):
    return lax.dot_general(
        left_side, right_side, (((0,), (0,)), ((), ())), preferred_element_type=jnp.float32
    )


def on_device(
    tokens, out_grad, counts, block_moves, segment_ids, gate_weight, up_weight, down_weight
):
    ranks_all = lax.axis_size(ROW)
    me_rank = lax.axis_index(ROW)
    slot_rows = tokens.shape[0]
    cap_blocks = slot_rows // BLOCK
    feat_cols = tokens.shape[1]
    my_count = counts[0]
    places = jnp.arange(slot_rows, dtype=jnp.int32)
    following = jnp.concatenate([segment_ids[1:], segment_ids[-1:]])
    own_weight = ((places + 1 < my_count) & (following == segment_ids)).astype(jnp.float32)
    source = block_moves[:, 0]
    target = block_moves[:, 1]
    block_id = block_moves[:, 2]
    block_ids = jnp.arange(cap_blocks, dtype=jnp.int32)
    filled = (my_count + BLOCK - 1) // BLOCK
    moved_out = jnp.any(
        (source[None, :] == me_rank) & (block_id[None, :] == block_ids[:, None]), axis=1
    )
    kept_flag = (block_ids < filled) & jnp.logical_not(moved_out)
    arrive = target == me_rank
    flag_bits = jnp.concatenate([kept_flag, arrive]).astype(jnp.int32)
    local_ids = jnp.concatenate([block_ids, cap_blocks + source])
    list_place = jnp.cumsum(flag_bits) - 1
    slot_ids = jnp.arange(WORK, dtype=jnp.int32)
    slot_hit = (flag_bits[:, None] == 1) & (list_place[:, None] == slot_ids[None, :])
    slot_index = jnp.sum(jnp.where(slot_hit, local_ids[:, None] + 1, 0), axis=0) - 1
    peer_ids = jnp.arange(ranks_all, dtype=jnp.int32)
    outgoing = (source[None, :] == me_rank) & (target[None, :] == peer_ids[:, None])
    send_block = jnp.sum(jnp.where(outgoing, block_id[None, :], 0), axis=1)
    send_live = jnp.any(outgoing, axis=1)
    own_tokens = tokens.reshape(cap_blocks, BLOCK, feat_cols)
    own_grad = out_grad.reshape(cap_blocks, BLOCK, feat_cols)
    own_mask = own_weight.astype(jnp.bfloat16).reshape(cap_blocks, BLOCK)

    def outbox(block_rows):
        chosen = jnp.take(block_rows, send_block, axis=0)
        live_rows = send_live.reshape((-1,) + (1,) * (chosen.ndim - 1))
        return jnp.where(live_rows, chosen, jnp.zeros_like(chosen))

    whole_count = jnp.sum(own_weight).astype(jnp.int32)
    count_parts = jnp.broadcast_to(
        jnp.stack([whole_count // 256, whole_count % 256]).astype(jnp.bfloat16)[None, :],
        (ranks_all, 2),
    )
    got_tokens, got_grad, got_mask, got_parts = (
        lax.all_to_all(outbox(own_tokens), ROW, split_axis=0, concat_axis=0, tiled=True),
        lax.all_to_all(outbox(own_grad), ROW, split_axis=0, concat_axis=0, tiled=True),
        lax.all_to_all(outbox(own_mask), ROW, split_axis=0, concat_axis=0, tiled=True),
        lax.all_to_all(count_parts, ROW, split_axis=0, concat_axis=0, tiled=True),
    )
    part_values = got_parts.astype(jnp.float32)
    loss_total = 256.0 * jnp.sum(part_values[:, 0]) + jnp.sum(part_values[:, 1])

    def to_work(pool_rows):
        chosen = jnp.take(pool_rows, jnp.maximum(slot_index, 0), axis=0)
        live_rows = (slot_index >= 0).reshape((-1,) + (1,) * (chosen.ndim - 1))
        return jnp.where(live_rows, chosen, jnp.zeros_like(chosen))

    work_tokens = to_work(jnp.concatenate([own_tokens, got_tokens])).reshape(
        WORK * BLOCK, feat_cols
    )
    work_grad = to_work(jnp.concatenate([own_grad, got_grad])).reshape(WORK * BLOCK, feat_cols)
    work_mask = to_work(jnp.concatenate([own_mask, got_mask])).reshape(WORK * BLOCK)
    work_weight = work_mask.astype(jnp.float32)
    full_tokens, full_grad = side_by_side((work_tokens, work_grad), "col", 1, 0)
    hidden_cols = gate_weight.shape[1]
    gate_piece, up_piece, down_piece = side_by_side(
        (gate_weight, up_weight, down_weight), ROW, 0, 1
    )
    gate_sum = jnp.dot(full_tokens, gate_piece, preferred_element_type=jnp.float32)
    up_sum = jnp.dot(full_tokens, up_piece, preferred_element_type=jnp.float32)
    back_raw = jnp.dot(full_grad, down_piece, preferred_element_type=jnp.float32)
    back_sum = back_raw * work_weight[:, None]
    hidden, gate_back, up_back = local_terms(gate_sum, up_sum, back_sum)
    weighted = full_grad * work_mask[:, None]

    def term_rows(left_side, right_side):
        return contract(left_side, right_side) / loss_total

    joined = own_rows(
        jnp.concatenate(
            [
                term_rows(full_tokens, gate_back),
                term_rows(full_tokens, up_back),
                term_rows(weighted, hidden),
            ],
            axis=1,
        ),
        ROW,
    )
    gate_grad = joined[:, :hidden_cols]
    up_grad = joined[:, hidden_cols : 2 * hidden_cols]
    down_grad = joined[:, 2 * hidden_cols :]
    return (hidden, gate_grad, up_grad, down_grad)


def solution(mesh):
    torus = Mesh(mesh.devices.reshape(8, 4, mesh.shape["col"]), ("row_0", "row_1", "col"))
    return jax.shard_map(
        on_device,
        mesh=torus,
        in_specs=(
            P(ROW, "col"),
            P(ROW, "col"),
            P(ROW),
            P(),
            P(ROW),
            P(ROW, "col"),
            P(ROW, "col"),
            P(ROW, "col"),
        ),
        out_specs=(P(ROW, "col"), P(ROW, "col"), P(ROW, "col"), P(ROW, "col")),
        check_vma=False,
    )
```

profile of v0, /device:TPU:8, one launch (start us, length us, event | category | flops | bytes accessed | tf_op | source)
XLA Modules:
  0.0 372.3 jit_solution(14221137799837593401)
XLA Ops:
  7.2 0.8 add_bitcast_fusion
  8.0 0.8 slice_compare_fusion
  8.9 1.7 gather_fusion.4
  10.6 1.7 gather_fusion.2
  12.3 1.3 select_select_fusion.1
  13.7 37.3 %all_to_all.25 = bf16[32,128,128]{2,1,0:T(8,128)(2,1)S(1)} all-to-all(bf16[32,128,128]{2,1,0:T(8,128)(2,1)S(1)} %get-tuple-element.47), channel_id=1, replica_groups=mesh['row_0'=8,'row_1'=4,'col'=16] {'row_0','row_1'}, dimensions={0} | all-to-all | bytes 2097152 | tf_op jit(solution)/shard_map/all_to_all | solution.py:93
  50.9 6.6 %all-to-all-start = ((bf16[32,128,128]{2,1,0:T(8,128)(2,1)}), bf16[32,128,128]{2,1,0:T(8,128)(2,1)S(1)}, u32[]{:S(2)}, u32[]{:S(2)}) async-start(bf16[32,128,128]{2,1,0:T(8,128)(2,1)} %get-tuple-element.46), calls=%async_computation | async-start | bytes 2097152 | tf_op jit(solution)/shard_map/all_to_all | solution.py:92
  59.1 1.2 pad_maximum_fusion.2
  60.2 1.9 gather_fusion.5
  62.1 21.9 %all-to-all-done = bf16[32,128,128]{2,1,0:T(8,128)(2,1)S(1)} async-done(((bf16[32,128,128]{2,1,0:T(8,128)(2,1)}), bf16[32,128,128]{2,1,0:T(8,128)(2,1)S(1)}, u32[]{:S(2)}, u32[]{:S(2)}) %all-to-all-start) | async-done | bytes 1048608 | tf_op jit(solution)/shard_map/all_to_all | solution.py:92
  84.8 0.7 pad_maximum_fusion.3
  87.0 0.7 fusion.28
  89.7 6.1 %all-to-all-start.3 = ((bf16[32,1,2]{2,1,0:T(2,128)(2,1)}), bf16[32,1,2]{2,1,0:T(2,128)(2,1)S(1)}, u32[]{:S(2)}, u32[]{:S(2)}) async-start(bf16[32,1,2]{2,1,0:T(2,128)(2,1)} %broadcast_in_dim.133), calls=%async_computation.3 | async-start | bytes 32768 | tf_op jit(solution)/shard_map/all_to_all | solution.py:95
  97.2 7.2 %all-to-all-done.3 = bf16[32,1,2]{2,1,0:T(2,128)(2,1)S(1)} async-done(((bf16[32,1,2]{2,1,0:T(2,128)(2,1)}), bf16[32,1,2]{2,1,0:T(2,128)(2,1)S(1)}, u32[]{:S(2)}, u32[]{:S(2)}) %all-to-all-start.3) | async-done | bytes 160 | tf_op jit(solution)/shard_map/all_to_all | solution.py:95
  104.4 4.9 %all-to-all-start.2 = ((bf16[32,1,128]{2,1,0:T(2,128)(2,1)}), bf16[32,1,128]{2,1,0:T(2,128)(2,1)S(1)}, u32[]{:S(2)}, u32[]{:S(2)}) async-start(bf16[32,1,128]{2,1,0:T(2,128)(2,1)} %copy.39), calls=%async_computation.2 | async-start | bytes 32768 | tf_op jit(solution)/shard_map/all_to_all | solution.py:94
  111.5 6.4 %all-to-all-done.2 = bf16[32,1,128]{2,1,0:T(2,128)(2,1)S(1)} async-done(((bf16[32,1,128]{2,1,0:T(2,128)(2,1)}), bf16[32,1,128]{2,1,0:T(2,128)(2,1)S(1)}, u32[]{:S(2)}, u32[]{:S(2)}) %all-to-all-start.2) | async-done | bytes 8224 | tf_op jit(solution)/shard_map/all_to_all | solution.py:94
  118.5 19.9 %all-gather.3.cloned.1.call-done = bf16[1024,2048]{1,0:T(8,128)(2,1)} async-done(((bf16[1024,128]{1,0:T(8,128)(2,1)}), bf16[1024,2048]{1,0:T(8,128)(2,1)}) %all-gather.3.cloned.1.call-update) | async-done | bytes 4194320 | tf_op jit(solution)/shard_map/all_gather | solution.py:14
  138.4 95.2 %all-gather.5.cloned.1.call-done = bf16[2048,1536]{1,0:T(8,128)(2,1)} async-done(((bf16[64,1536]{1,0:T(8,128)(2,1)}), bf16[2048,1536]{1,0:T(8,128)(2,1)}) %all-gather.5.cloned.1.call-update) | async-done | bytes 6291472 | tf_op jit(solution)/shard_map/all_gather | solution.py:14
  233.6 3.6 fusion.4
  237.7 3.0 fusion.13
  240.7 1.4 multiply_convert_fusion.2
  242.0 1.4 divide_convert_fusion.1
  243.4 1.5 divide_convert_fusion.2
  245.0 1.4 divide_convert_fusion
  246.4 11.3 %pad_maximum_fusion = bf16[2048,1536]{0,1:T(8,128)(2,1)} fusion(bf16[2048,512]{0,1:T(8,128)(2,1)S(1)} %divide_convert_fusion, bf16[2048,512]{0,1:T(8,128)(2,1)S(1)} %divide_convert_fusion.1, bf16[2048,512]{0,1:T(8,128)(2,1)S(1)} %divide_convert_fusion.2), kind=kLoop, calls=%fused_computation.6 | loop fusion | flops 18874368 | bytes 12582912 | tf_op jit(solution)/shard_map/concatenate | solution.py:127
  257.7 73.4 %reduce-scatter.5.cloned.1.call-done = bf16[256,1536]{0,1:T(8,128)(2,1)} async-done(((bf16[2048,1536]{0,1:T(8,128)(2,1)}), bf16[256,1536]{0,1:T(8,128)(2,1)}) %reduce-scatter.5.cloned.1.call-update) | async-done | bytes 786448 | tf_op jit(solution)/shard_map/reduce_scatter | solution.py:24
  331.1 2.3 copy.44
  333.4 28.8 %reduce-scatter.7.cloned.1.call-done = bf16[64,1536]{1,0:T(8,128)(2,1)} async-done(((bf16[256,1536]{1,0:T(8,128)(2,1)}), bf16[64,1536]{1,0:T(8,128)(2,1)}) %reduce-scatter.7.cloned.1.call-update) | async-done | bytes 196624
  362.2 1.1 copy.45
  363.4 0.8 copy.43
  364.2 0.8 copy.42
  365.0 0.8 copy.41
  (67 shorter events, 8.0 us)
Async XLA Ops:
  12.3 46.7 %copy-start = (bf16[768,128]{1,0:T(8,128)(2,1)S(1)}, bf16[768,128]{1,0:T(8,128)(2,1)}, u32[]{:S(2)}) copy-start(bf16[768,128]{1,0:T(8,128)(2,1)} %param.13) | copy-start | bytes 589828
  13.7 70.3 %copy-start.1 = (bf16[768,128]{1,0:T(8,128)(2,1)S(1)}, bf16[768,128]{1,0:T(8,128)(2,1)}, u32[]{:S(2)}) copy-start(bf16[768,128]{1,0:T(8,128)(2,1)} %param.12) | copy-start | bytes 589828
  50.9 34.7 %copy-start.2 = (bf16[64,512]{1,0:T(8,128)(2,1)S(1)}, bf16[64,512]{1,0:T(8,128)(2,1)}, u32[]{:S(2)}) copy-start(bf16[64,512]{1,0:T(8,128)(2,1)} %param.19) | copy-start | bytes 196612
  50.9 34.7 %copy-start.3 = (bf16[64,512]{1,0:T(8,128)(2,1)S(1)}, bf16[64,512]{1,0:T(8,128)(2,1)}, u32[]{:S(2)}) copy-start(bf16[64,512]{1,0:T(8,128)(2,1)} %param.18) | copy-start | bytes 196612
  50.9 34.7 %copy-start.4 = (bf16[64,512]{1,0:T(8,128)(2,1)S(1)}, bf16[64,512]{1,0:T(8,128)(2,1)}, u32[]{:S(2)}) copy-start(bf16[64,512]{1,0:T(8,128)(2,1)} %param.17) | copy-start | bytes 196612
  50.9 33.1 %all-to-all-start = ((bf16[32,128,128]{2,1,0:T(8,128)(2,1)}), bf16[32,128,128]{2,1,0:T(8,128)(2,1)S(1)}, u32[]{:S(2)}, u32[]{:S(2)}) async-start(bf16[32,128,128]{2,1,0:T(8,128)(2,1)} %get-tuple-element.46), calls=%async_computation | async-start | bytes 2097152 | tf_op jit(solution)/shard_map/all_to_all | solution.py:92
  57.5 28.8 %copy-start.5 = (s32[768]{0:T(1024)S(1)}, s32[768]{0:T(1024)}, u32[]{:S(2)}) copy-start(s32[768]{0:T(1024)} %param.16) | copy-start | bytes 9220
  57.5 80.9 %all-gather.3.cloned.1.call-start = ((), (), s32[]{:S(2)}) async-start(), calls=%async_computation.6 | async-start | bytes 4456448 | tf_op jit(solution)/shard_map/all_gather | solution.py:14
  85.6 148.0 %all-gather.5.cloned.1.call-start = ((), (), s32[]{:S(2)}) async-start(), calls=%async_computation.7 | async-start | bytes 6488064 | tf_op jit(solution)/shard_map/all_gather | solution.py:14
  89.7 14.6 %all-to-all-start.3 = ((bf16[32,1,2]{2,1,0:T(2,128)(2,1)}), bf16[32,1,2]{2,1,0:T(2,128)(2,1)S(1)}, u32[]{:S(2)}, u32[]{:S(2)}) async-start(bf16[32,1,2]{2,1,0:T(2,128)(2,1)} %broadcast_in_dim.133), calls=%async_computation.3 | async-start | bytes 32768 | tf_op jit(solution)/shard_map/all_to_all | solution.py:95
  104.4 13.5 %all-to-all-start.2 = ((bf16[32,1,128]{2,1,0:T(2,128)(2,1)}), bf16[32,1,128]{2,1,0:T(2,128)(2,1)S(1)}, u32[]{:S(2)}, u32[]{:S(2)}) async-start(bf16[32,1,128]{2,1,0:T(2,128)(2,1)} %copy.39), calls=%async_computation.2 | async-start | bytes 32768 | tf_op jit(solution)/shard_map/all_to_all | solution.py:94
  109.3 221.8 %reduce-scatter.5.cloned.1.call-start = ((), (), s32[]{:S(2)}) async-start(), calls=%async_computation.8 | async-start | bytes 7077888 | tf_op jit(solution)/shard_map/reduce_scatter | solution.py:24
  233.6 4.1 %copy-start.6 = (bf16[2048,1536]{1,0:T(8,128)(2,1)S(1)}, bf16[2048,1536]{1,0:T(8,128)(2,1)}, u32[]{:S(2)}) copy-start(bf16[2048,1536]{1,0:T(8,128)(2,1)} %all-gather.5.cloned.1.call-done) | copy-start | bytes 18874372
  237.7 3.0 copy-start.7
  242.0 3.0 copy-start.8
  257.7 104.5 %reduce-scatter.7.cloned.1.call-start = ((), (), s32[]{:S(2)}) async-start(), calls=%async_computation.9 | async-start | bytes 983040
Sparse Core Ops, SparseCore 0:
  85.7 52.6 all-gather.2
  141.6 91.9 all-gather.4
  257.8 73.2 reduce-scatter.4
  333.8 28.3 reduce-scatter.6
where the time goes:
time: 373 us; the launch traced here: 372 us
  waiting for transfers between devices  253 us (68%)
  blocking collectives  37.3 us (10%)
  other arithmetic  20 us (5%)
  starting transfers between devices  17.9 us (5%)
  between operations  16.7 us (4%)
  local copies, waits for them, and re-layouts  15.3 us (4%)
  matrix products  12.3 us (3%)
    all_gather x2, waiting for transfers between devices, side_by_side(): filled, at, outs = (lax.all_gather(both, axis, axis=dim, tiled=True), 0, [])  115 us
    reduce_scatter x1, waiting for transfers between devices, own_rows(): running = lax.psum_scatter(running, axis, scatter_dimension=0, tiled=True)  73.4 us
    all_to_all x1, blocking collectives, on_device(): lax.all_to_all(outbox(own_grad), ROW, split_axis=0, concat_axis=0, tiled=...  37.3 us
    unnamed x5, waiting for transfers between devices  28.8 us
    all_to_all x1, waiting for transfers between devices, on_device(): lax.all_to_all(outbox(own_tokens), ROW, split_axis=0, concat_axis=0, tile...  21.9 us
    concatenate x1, other arithmetic, on_device(): jnp.concatenate([term_rows(full_tokens, gate_back), term_rows(full_tokens...  11.3 us
  transfers between devices with their start and end apart: 7, of which 7 were waited for; matrix products, arithmetic and copies ran while one was open for 3% of the time, Pallas kernels for 0%

commit v1 on v0

v1 whole, which is shorter than its diff:
```python
import jax
import jax.numpy as jnp
from jax import lax
from jax.experimental import pallas as pl
from jax.experimental.pallas import tpu as pltpu
from jax.sharding import Mesh
from jax.sharding import PartitionSpec as P

BLOCK = 128
WORK = 4
CAP = 6
NY, NX, NZ = 8, 4, 8
ROW = ("y", "x")
COL = ("z", "c")
NTAG = 16
SIDE = 768


def vmem():
    return pl.BlockSpec(memory_space=pltpu.VMEM)


def smem():
    return pl.BlockSpec(memory_space=pltpu.SMEM)


def params(**kw):
    return pltpu.CompilerParams(vmem_limit_bytes=60 * 1024 * 1024, **kw)


def move_count(moves):
    return moves.shape[0] // 3


def pack_x(pos, moves, mask, tok, grad, box, masked):
    me = pos[0] * NX + pos[1]
    for b in range(CAP):
        rows = slice(b * BLOCK, (b + 1) * BLOCK)
        wide = jnp.broadcast_to(mask[b : b + 1, :], (BLOCK, BLOCK)).T
        masked[rows, :] = (grad[rows, :].astype(jnp.float32) * wide).astype(jnp.bfloat16)
    tally = jnp.sum(mask[...], axis=0, keepdims=True)
    for d in range(NX):
        box[d, 4 * BLOCK :, :] = jnp.broadcast_to(tally, (NTAG, BLOCK)).astype(jnp.bfloat16)

    def body(m, seen):
        src, dst, blk = moves[3 * m], moves[3 * m + 1], moves[3 * m + 2]
        mine = src == me

        @pl.when(mine)
        def _():
            peer = dst % NX
            at = pl.multiple_of(seen * (2 * BLOCK), BLOCK)
            start = pl.multiple_of(blk * BLOCK, BLOCK)
            box[peer, pl.ds(at, BLOCK), :] = tok[pl.ds(start, BLOCK), :]
            box[peer, pl.ds(at + BLOCK, BLOCK), :] = masked[pl.ds(start, BLOCK), :]

        return jnp.where(mine, jnp.minimum(seen + 1, 1), seen)

    lax.fori_loop(0, move_count(moves), body, 0)


def pack_y(pos, moves, got, box, seen):
    my, mx = pos[0], pos[1]
    for i in range(NX):
        seen[i] = 0
    tally = got[0, 4 * BLOCK :, :].astype(jnp.float32)
    for i in range(1, NX):
        tally = tally + got[i, 4 * BLOCK :, :].astype(jnp.float32)
    for d in range(NY):
        box[d, 2 * BLOCK :, :] = tally.astype(jnp.bfloat16)

    def body(m, carry):
        src, dst = moves[3 * m], moves[3 * m + 1]

        @pl.when(src // NX == my)
        def _():
            sx = src % NX
            nth = seen[sx]
            seen[sx] = jnp.minimum(nth + 1, 1)

            @pl.when(dst % NX == mx)
            def _():
                at = pl.multiple_of(nth * (2 * BLOCK), BLOCK)
                box[dst // NX, : 2 * BLOCK, :] = got[sx, pl.ds(at, 2 * BLOCK), :]

        return carry

    lax.fori_loop(0, move_count(moves), body, 0)


def fill_work(pos, moves, tok, masked, got, box, total):
    me = pos[0] * NX + pos[1]
    count = pos[2]
    span = WORK * BLOCK
    tally = got[0, 2 * BLOCK : 2 * BLOCK + 8, :].astype(jnp.float32)
    for i in range(1, NY):
        tally = tally + got[i, 2 * BLOCK : 2 * BLOCK + 8, :].astype(jnp.float32)
    total[...] = jnp.broadcast_to(jnp.sum(tally, axis=1, keepdims=True), total.shape)
    box[0] = jnp.zeros_like(box[0])

    def put(slot, t, g):
        at = pl.multiple_of(slot * BLOCK, BLOCK)
        box[0, pl.ds(at, BLOCK), :] = t
        box[0, pl.ds(at + span, BLOCK), :] = g

    def own(b, nth):
        def gone(m, hit):
            return hit | ((moves[3 * m] == me) & (moves[3 * m + 2] == b)).astype(jnp.int32)

        left = lax.fori_loop(0, move_count(moves), gone, 0)
        keep = (b * BLOCK < count) & (left == 0)

        @pl.when(keep & (nth < WORK))
        def _():
            start = pl.multiple_of(b * BLOCK, BLOCK)
            put(nth, tok[pl.ds(start, BLOCK), :], masked[pl.ds(start, BLOCK), :])

        return nth + keep.astype(jnp.int32)

    nth = lax.fori_loop(0, CAP, own, 0)

    def came(m, nth):
        src, dst = moves[3 * m], moves[3 * m + 1]
        here = dst == me

        @pl.when(here & (nth < WORK))
        def _():
            sy = src // NX
            put(nth, got[sy, :BLOCK, :], got[sy, BLOCK : 2 * BLOCK, :])

        return nth + here.astype(jnp.int32)

    lax.fori_loop(0, move_count(moves), came, nth)
    for d in range(1, NZ):
        box[d] = box[0]


def forward(pos, mine, other, wg, wu, wd, hidden, gate_back, up_back, tok, grad):
    span = WORK * BLOCK

    @pl.when(pl.program_id(0) == 0)
    def _():
        first = pos[3] == 0
        for z in range(NZ):
            a, b = mine[z], other[z]
            low = jnp.where(first, a, b)
            high = jnp.where(first, b, a)
            at = z * 2 * BLOCK
            tok[:, at : at + BLOCK] = low[:span]
            grad[:, at : at + BLOCK] = low[span:]
            tok[:, at + BLOCK : at + 2 * BLOCK] = high[:span]
            grad[:, at + BLOCK : at + 2 * BLOCK] = high[span:]

    gate_sum = jnp.dot(tok[...], wg[...], preferred_element_type=jnp.float32)
    up_sum = jnp.dot(tok[...], wu[...], preferred_element_type=jnp.float32)
    back_sum = jnp.dot(grad[...], wd[...], preferred_element_type=jnp.float32)
    logistic = jax.nn.sigmoid(gate_sum)
    act = gate_sum * logistic
    hidden[...] = (act * up_sum).astype(jnp.bfloat16)
    gate_back[...] = (back_sum * up_sum * logistic * (1.0 + gate_sum * (1.0 - logistic))).astype(
        jnp.bfloat16
    )
    up_back[...] = (back_sum * act).astype(jnp.bfloat16)


def gradients(total, tok, grad, hidden, gate_back, up_back, by_x, by_y):
    inv = 1.0 / total[0, 0]

    def term(left, right):
        out = lax.dot_general(
            left, right, (((0,), (0,)), ((), ())), preferred_element_type=jnp.float32
        )
        return (out * inv).astype(jnp.bfloat16)

    half = 256
    t, g = tok[...], grad[...]
    gate = term(t, gate_back[...])
    up = term(t, up_back[...])
    down = term(g, hidden[...])
    for x in range(NX):
        rows = slice(64 * x, 64 * (x + 1))
        by_x[x, 0, :, :512] = gate[rows]
        by_x[x, 0, :, 512:] = up[rows, :half]
    by_y[0, :, :half] = up[:, half:]
    by_y[0, :, half:] = down


def add_x(got, out):
    acc = got[0].astype(jnp.float32)
    for i in range(1, NX):
        acc = acc + got[i].astype(jnp.float32)
    out[...] = acc.astype(jnp.bfloat16)


def finish(from_y, from_x, gate, up, down):
    acc = from_y[0].astype(jnp.float32)
    for i in range(1, NY):
        acc = acc + from_y[i].astype(jnp.float32)
    bcc = from_x[0].astype(jnp.float32)
    for i in range(1, NX):
        bcc = bcc + from_x[i].astype(jnp.float32)
    gate[...] = acc[:, :512]
    up[:, :256] = acc[:, 512:]
    up[:, 256:] = bcc[:, :256]
    down[...] = bcc[:, 256:]


def a2a(value, axis):
    return lax.all_to_all(value, axis, split_axis=0, concat_axis=0, tiled=True)


def on_device(
    tokens, out_grad, counts, block_moves, segment_ids, gate_weight, up_weight, down_weight
):
    bf = jnp.bfloat16
    f32 = jnp.float32
    slots = tokens.shape[0]
    feat = tokens.shape[1]
    hid = gate_weight.shape[1]
    span = WORK * BLOCK
    model = 2 * NZ * feat
    weights = lax.all_gather(
        jnp.concatenate([gate_weight, up_weight, down_weight], axis=1), ROW, axis=0, tiled=True
    )

    count = counts[0]
    pos = jnp.stack([lax.axis_index("y"), lax.axis_index("x"), count, lax.axis_index("c")])
    moves = block_moves.reshape(-1)
    places = jnp.arange(slots, dtype=jnp.int32)
    following = jnp.concatenate([segment_ids[1:], segment_ids[-1:]])
    mask = ((places + 1 < count) & (following == segment_ids)).astype(f32).reshape(CAP, BLOCK)

    box, masked = pl.pallas_call(
        pack_x,
        out_shape=(
            jax.ShapeDtypeStruct((NX, 4 * BLOCK + NTAG, feat), bf),
            jax.ShapeDtypeStruct((slots, feat), bf),
        ),
        in_specs=[smem(), smem(), vmem(), vmem(), vmem()],
        out_specs=(vmem(), vmem()),
        compiler_params=params(),
        name="pack_x",
    )(pos, moves, mask, tokens, out_grad)
    got = a2a(box, "x")
    box = pl.pallas_call(
        pack_y,
        out_shape=jax.ShapeDtypeStruct((NY, 2 * BLOCK + NTAG, feat), bf),
        in_specs=[smem(), smem(), vmem()],
        out_specs=vmem(),
        scratch_shapes=[pltpu.SMEM((NX,), jnp.int32)],
        compiler_params=params(),
        name="pack_y",
    )(pos, moves, got)
    got = a2a(box, "y")
    box, total = pl.pallas_call(
        fill_work,
        out_shape=(
            jax.ShapeDtypeStruct((NZ, 2 * span, feat), bf),
            jax.ShapeDtypeStruct((8, BLOCK), f32),
        ),
        in_specs=[smem(), smem(), vmem(), vmem(), vmem()],
        out_specs=(vmem(), vmem()),
        compiler_params=params(),
        name="fill_work",
    )(pos, moves, tokens, masked, got)
    mine = a2a(box, "z")
    other = lax.ppermute(mine, "c", [(0, 1), (1, 0)])

    tile = 256
    steps = hid // tile

    def whole(shape):
        return pl.BlockSpec(shape, lambda j: (0,) * len(shape))

    def cols(rows, offset):
        return pl.BlockSpec((rows, tile), lambda j: (0, j + offset))

    hidden, gate_back, up_back, tok, grad = pl.pallas_call(
        forward,
        grid=(steps,),
        out_shape=(
            jax.ShapeDtypeStruct((span, hid), bf),
            jax.ShapeDtypeStruct((span, hid), bf),
            jax.ShapeDtypeStruct((span, hid), bf),
            jax.ShapeDtypeStruct((span, model), bf),
            jax.ShapeDtypeStruct((span, model), bf),
        ),
        in_specs=[
            smem(),
            whole((NZ, 2 * span, feat)),
            whole((NZ, 2 * span, feat)),
            cols(model, 0),
            cols(model, steps),
            cols(model, 2 * steps),
        ],
        out_specs=(
            cols(span, 0),
            cols(span, 0),
            cols(span, 0),
            whole((span, model)),
            whole((span, model)),
        ),
        compiler_params=params(dimension_semantics=("arbitrary",)),
        name="forward",
    )(pos, mine, other, weights, weights, weights)

    per = 64
    by_x, by_y = pl.pallas_call(
        gradients,
        grid=(NY,),
        out_shape=(
            jax.ShapeDtypeStruct((NX, NY, per, SIDE), bf),
            jax.ShapeDtypeStruct((NY, NX * per, SIDE), bf),
        ),
        in_specs=[
            pl.BlockSpec((8, BLOCK), lambda j: (0, 0)),
            pl.BlockSpec((span, NX * per), lambda j: (0, j)),
            pl.BlockSpec((span, NX * per), lambda j: (0, j)),
            whole((span, hid)),
            whole((span, hid)),
            whole((span, hid)),
        ],
        out_specs=(
            pl.BlockSpec((NX, 1, per, SIDE), lambda j: (0, j, 0, 0)),
            pl.BlockSpec((1, NX * per, SIDE), lambda j: (j, 0, 0)),
        ),
        compiler_params=params(dimension_semantics=("arbitrary",)),
        name="gradients",
    )(total, tok, grad, hidden, gate_back, up_back)

    part_y = lax.psum_scatter(
        by_y.reshape(NY * NX * per, SIDE), "y", scatter_dimension=0, tiled=True
    )
    part_x = pl.pallas_call(
        add_x,
        out_shape=jax.ShapeDtypeStruct((NY, per, SIDE), bf),
        in_specs=[vmem()],
        out_specs=vmem(),
        compiler_params=params(),
        name="add_x",
    )(a2a(by_x, "x"))
    from_y = a2a(part_x, "y")
    from_x = a2a(part_y.reshape(NX, per, SIDE), "x")
    gate_grad, up_grad, down_grad = pl.pallas_call(
        finish,
        out_shape=tuple(jax.ShapeDtypeStruct((per, hid), f32) for _ in range(3)),
        in_specs=[vmem(), vmem()],
        out_specs=(vmem(), vmem(), vmem()),
        compiler_params=params(),
        name="finish",
    )(from_y, from_x)
    return (hidden, gate_grad, up_grad, down_grad)


def solution(mesh):
    torus = Mesh(mesh.devices.reshape(NY, NX, NZ, 2), ("y", "x", "z", "c"))
    return jax.shard_map(
        on_device,
        mesh=torus,
        in_specs=(P(ROW, COL), P(ROW, COL), P(ROW), P(), P(ROW), P(ROW, COL), P(ROW, COL), P(ROW, COL)),
        out_specs=(P(ROW, COL), P(ROW, COL), P(ROW, COL), P(ROW, COL)),
        check_vma=False,
    )
```

time: 373 us -> 244 us (0.65)
  the two profiles are of different devices: /device:TPU:8 before, /device:TPU:2 now
where the time goes in v1:
time: 244 us; the launch traced here: 243 us
  blocking collectives  180 us (74%)
  Pallas kernels  32.4 us (13%)
  between operations  14.7 us (6%)
  local copies, waits for them, and re-layouts  5.33 us (2%)
  waiting for transfers between devices  4.29 us (2%)
  other arithmetic  4.19 us (2%)
    all_to_all x6, blocking collectives, a2a(): return lax.all_to_all(value, axis, split_axis=0, concat_axis=0, tiled=True)  180 us
    pallas_call x1, Pallas kernels, on_device(): pl.pallas_call(gradients, grid=(NY,), out_shape=(jax.ShapeDtypeStruct((NX...  9.61 us
    pallas_call x1, Pallas kernels, on_device(): pl.pallas_call(forward, grid=(steps,), out_shape=(jax.ShapeDtypeStruct((s...  8.94 us
  transfers between devices with their start and end apart: 3, of which 1 were waited for; matrix products, arithmetic and copies ran while one was open for 2% of the time, Pallas kernels for 5%

profile of v1, /device:TPU:2, one launch (start us, length us, event | category | flops | bytes accessed | tf_op | source)
XLA Modules:
  0.0 243.4 jit_solution(9259100764587657381)
XLA Ops:
  7.2 0.0 all-gather.2.cloned.1.call-start
  7.2 1.6 pad_maximum_fusion
  8.8 0.0 all-gather.2.cloned.1.call-update
  8.8 0.0 reduce-scatter.2.cloned.1.call-start
  8.9 1.3 slice.7
  10.2 0.8 slice.6
  11.6 0.8 copy.13
  12.4 0.6 reshape.22.moves
  13.0 0.6 pad_add_fusion.pos
  13.6 2.0 convert_bitcast_fusion.mask
  15.6 2.3 pack_x.1
  17.9 17.0 %all_to_all.30.got = bf16[4,528,128]{2,1,0:T(8,128)(2,1)} all-to-all(bf16[4,528,128]{2,1,0:T(8,128)(2,1)} %get-tuple-element.19), channel_id=1, replica_groups=mesh['y'=8,'x'=4,'z'=8,'c'=2] {'x'}, dimensions={0} | all-to-all | bytes 1081344 | tf_op jit(solution)/shard_map/all_to_all | solution.py:209
  34.9 2.3 pack_y.1
  37.2 24.3 %all_to_all.31.got = bf16[8,272,128]{2,1,0:T(8,128)(2,1)} all-to-all(bf16[8,272,128]{2,1,0:T(8,128)(2,1)} %pack_y.1), channel_id=1, replica_groups=mesh['y'=8,'x'=4,'z'=8,'c'=2] {'y'}, dimensions={0} | all-to-all | bytes 1114112 | tf_op jit(solution)/shard_map/all_to_all | solution.py:209
  61.5 4.1 %fill_work.1 = (bf16[8,1024,128]{2,1,0:T(8,128)(2,1)}, f32[8,128]{1,0:T(8,128)}) custom-call(s32[4]{0:T(128)} %pad_add_fusion.pos, s32[48]{0:T(128)} %reshape.22.moves, bf16[768,128]{1,0:T(8,128)(2,1)} %tok.3, bf16[768,128]{1,0:T(8,128)(2,1)} %get-tuple-element.18.masked, bf16[8,272,128]{2,1,0:T(8,128)(2,1)} %all_to_all.31.got), custom_call_target="tpu_custom_call" | custom-call | tf_op jit(solution)/shard_map/fill_work/pallas_call | solution.py:255
  65.5 58.8 %all_to_all.32.mine = bf16[8,1024,128]{2,1,0:T(8,128)(2,1)S(1)} all-to-all(bf16[8,1024,128]{2,1,0:T(8,128)(2,1)} %get-tuple-element.20), channel_id=1, replica_groups=mesh['y'=8,'x'=4,'z'=8,'c'=2] {'z'}, dimensions={0} | all-to-all | bytes 4194304 | tf_op jit(solution)/shard_map/all_to_all | solution.py:209
  124.4 0.0 copy-start
  124.4 1.9 collective-permute-start
  126.3 4.3 %collective-permute-done.other = bf16[8,1024,128]{2,1,0:T(8,128)(2,1)} collective-permute-done((bf16[8,1024,128]{2,1,0:T(8,128)(2,1)S(1)}, bf16[8,1024,128]{2,1,0:T(8,128)(2,1)}, u32[]{:S(2)}, u32[]{:S(2)}) %collective-permute-start) | collective-permute-done | bytes 2097184 | tf_op jit(solution)/shard_map/ppermute | solution.py:267
  130.6 0.0 all-gather.2.cloned.1.call-done.wg.wu.wd
  130.6 0.0 copy-done
  130.6 8.9 %forward.1 = (bf16[512,512]{1,0:T(8,128)(2,1)}, bf16[512,512]{1,0:T(8,128)(2,1)}, bf16[512,512]{1,0:T(8,128)(2,1)}, bf16[512,2048]{1,0:T(8,128)(2,1)}, bf16[512,2048]{1,0:T(8,128)(2,1)}) custom-call(s32[4]{0:T(128)} %pad_add_fusion.pos, bf16[8,1024,128]{2,1,0:T(8,128)(2,1)} %copy-done, bf16[8,1024,128]{2,1,0:T(8,128)(2,1)} %collective-permute-done.other, ...), custom_call_target="tpu_custom_call" | custom-call | tf_op jit(solution)/shard_map/forward/pallas_call | solution.py:278
  139.5 9.6 %gradients.1 = (bf16[4,8,64,768]{3,2,1,0:T(8,128)(2,1)}, bf16[8,256,768]{2,1,0:T(8,128)(2,1)}) custom-call(f32[8,128]{1,0:T(8,128)} %get-tuple-element.22.total, bf16[512,2048]{1,0:T(8,128)(2,1)} %get-tuple-element.23.tok, bf16[512,2048]{1,0:T(8,128)(2,1)} %get-tuple-element.24.grad, bf16[512,512]{1,0:T(8,128)(2,1)} %get-tuple-element.14.hidden, ...), custom_call_target="tpu_custom_call" | custom-call | tf_op jit(solution)/shard_map/gradients/pallas_call | solution.py:308
  149.1 0.0 copy-start.1
  149.1 0.0 reduce-scatter.2.cloned.1.call-update
  149.1 1.9 copy-done.1
  151.0 41.7 %all_to_all.33.got = bf16[4,8,64,768]{3,2,1,0:T(8,128)(2,1)} all-to-all(bf16[4,8,64,768]{3,2,1,0:T(8,128)(2,1)S(1)} %copy-done.1), channel_id=1, replica_groups=mesh['y'=8,'x'=4,'z'=8,'c'=2] {'x'}, dimensions={0} | all-to-all | bytes 6291456 | tf_op jit(solution)/shard_map/all_to_all | solution.py:209
  192.7 3.2 %add_x.1 = bf16[8,64,768]{2,1,0:T(8,128)(2,1)} custom-call(bf16[4,8,64,768]{3,2,1,0:T(8,128)(2,1)} %all_to_all.33.got), custom_call_target="tpu_custom_call" | custom-call | tf_op jit(solution)/shard_map/add_x/pallas_call | solution.py:334
  195.9 27.0 %all_to_all.34.from_y = bf16[8,64,768]{2,1,0:T(8,128)(2,1)} all-to-all(bf16[8,64,768]{2,1,0:T(8,128)(2,1)} %add_x.1), channel_id=1, replica_groups=mesh['y'=8,'x'=4,'z'=8,'c'=2] {'y'}, dimensions={0} | all-to-all | bytes 1572864 | tf_op jit(solution)/shard_map/all_to_all | solution.py:209
  222.9 0.0 reduce-scatter.2.cloned.1.call-done
  222.9 11.6 %all_to_all.35.from_x = bf16[4,64,768]{2,1,0:T(8,128)(2,1)} all-to-all(bf16[4,64,768]{2,1,0:T(8,128)(2,1)} %bitcast.10), channel_id=1, replica_groups=mesh['y'=8,'x'=4,'z'=8,'c'=2] {'x'}, dimensions={0} | all-to-all | bytes 786432 | tf_op jit(solution)/shard_map/all_to_all | solution.py:209
  234.5 2.0 finish.1
Async XLA Ops:
  7.2 123.4 %all-gather.2.cloned.1.call-start = ((), (), s32[]{:S(2)}) async-start(), calls=%async_computation.7 | async-start | bytes 6488064 | tf_op jit(solution)/shard_map/all_gather | solution.py:222
  8.8 214.1 %reduce-scatter.2.cloned.1.call-start = ((), (), s32[]{:S(2)}) async-start(), calls=%async_computation.8 | async-start | bytes 3538944 | tf_op jit(solution)/shard_map/reduce_scatter | solution.py:331
  124.4 6.2 %copy-start = (bf16[8,1024,128]{2,1,0:T(8,128)(2,1)}, bf16[8,1024,128]{2,1,0:T(8,128)(2,1)S(1)}, u32[]{:S(2)}) copy-start(bf16[8,1024,128]{2,1,0:T(8,128)(2,1)S(1)} %all_to_all.32.mine) | copy-start | bytes 6291460
  124.4 6.2 %collective-permute-start = (bf16[8,1024,128]{2,1,0:T(8,128)(2,1)S(1)}, bf16[8,1024,128]{2,1,0:T(8,128)(2,1)}, u32[]{:S(2)}, u32[]{:S(2)}) collective-permute-start(bf16[8,1024,128]{2,1,0:T(8,128)(2,1)S(1)} %all_to_all.32.mine), channel_id=1, source_target_pairs={{0,1},{1,0},{2,3},{3,2},{4,5},{5,4},{6,7},{7,6},{8,9},{9,8},{10,11... | collective-permute-start | bytes 6291464 | tf_op jit(solution)/shard_map/ppermute | solution.py:267
  149.1 1.9 copy-start.1
Sparse Core Ops, SparseCore 0:
  11.1 99.8 all-gather.1
  149.3 41.2 reduce-scatter.1

commit v2 on v1

v2 whole, which is shorter than its diff:
```python
import jax
import jax.numpy as jnp
from jax import lax
from jax.experimental import pallas as pl
from jax.experimental.pallas import tpu as pltpu
from jax.sharding import Mesh
from jax.sharding import PartitionSpec as P

BLOCK = 128
WORK = 4
CAP = 6
NY, NX, NZ = 8, 4, 8
ROW = ("y", "x")
COL = ("z", "c")
NTAG = 16


def vmem():
    return pl.BlockSpec(memory_space=pltpu.VMEM)


def smem():
    return pl.BlockSpec(memory_space=pltpu.SMEM)


def params(**kw):
    return pltpu.CompilerParams(vmem_limit_bytes=60 * 1024 * 1024, **kw)


def move_count(moves):
    return moves.shape[1]


def pack_x(pos, moves, seg, tok, grad, box, work, masked):
    me = pos[0] * NX + pos[1]
    count = pos[2]
    span = WORK * BLOCK
    ids = seg[...]
    lane = lax.broadcasted_iota(jnp.int32, (CAP, BLOCK), 1)
    row = lax.broadcasted_iota(jnp.int32, (CAP, BLOCK), 0)
    ahead = jnp.concatenate([ids[1:], ids[-1:]], axis=0)
    joined = jnp.concatenate([ids[:, 1:], ahead[:, :1]], axis=1)
    mask = ((row * BLOCK + lane + 1 < count) & (joined == ids)).astype(jnp.float32)
    for b in range(CAP):
        rows = slice(b * BLOCK, (b + 1) * BLOCK)
        wide = jnp.broadcast_to(mask[b : b + 1, :], (BLOCK, BLOCK)).T
        masked[rows, :] = (grad[rows, :].astype(jnp.float32) * wide).astype(jnp.bfloat16)
    tally = jnp.sum(mask, axis=0, keepdims=True)
    for d in range(NX):
        box[d, 4 * BLOCK :, :] = jnp.broadcast_to(tally, (NTAG, BLOCK)).astype(jnp.bfloat16)

    def body(m, seen):
        src, dst, blk = moves[0, m], moves[1, m], moves[2, m]
        mine = src == me

        @pl.when(mine)
        def _():
            peer = dst % NX
            at = pl.multiple_of(seen * (2 * BLOCK), BLOCK)
            start = pl.multiple_of(blk * BLOCK, BLOCK)
            box[peer, pl.ds(at, BLOCK), :] = tok[pl.ds(start, BLOCK), :]
            box[peer, pl.ds(at + BLOCK, BLOCK), :] = masked[pl.ds(start, BLOCK), :]

        return jnp.where(mine, jnp.minimum(seen + 1, 1), seen)

    lax.fori_loop(0, move_count(moves), body, 0)
    work[0] = jnp.zeros_like(work[0])

    def own(b, nth):
        def gone(m, hit):
            return hit | ((moves[0, m] == me) & (moves[2, m] == b)).astype(jnp.int32)

        left = lax.fori_loop(0, move_count(moves), gone, 0)
        keep = (b * BLOCK < count) & (left == 0)

        @pl.when(keep & (nth < WORK))
        def _():
            start = pl.multiple_of(b * BLOCK, BLOCK)
            at = pl.multiple_of(nth * BLOCK, BLOCK)
            work[0, pl.ds(at, BLOCK), :] = tok[pl.ds(start, BLOCK), :]
            work[0, pl.ds(at + span, BLOCK), :] = masked[pl.ds(start, BLOCK), :]

        return nth + keep.astype(jnp.int32)

    lax.fori_loop(0, CAP, own, 0)
    for d in range(1, NZ):
        work[d] = work[0]


def pack_y(pos, moves, got, box, seen):
    my, mx = pos[0], pos[1]
    for i in range(NX):
        seen[i] = 0
    tally = got[0, 4 * BLOCK :, :].astype(jnp.float32)
    for i in range(1, NX):
        tally = tally + got[i, 4 * BLOCK :, :].astype(jnp.float32)
    for d in range(NY):
        box[d, 2 * BLOCK :, :] = tally.astype(jnp.bfloat16)

    def body(m, carry):
        src, dst = moves[0, m], moves[1, m]

        @pl.when(src // NX == my)
        def _():
            sx = src % NX
            nth = seen[sx]
            seen[sx] = jnp.minimum(nth + 1, 1)

            @pl.when(dst % NX == mx)
            def _():
                at = pl.multiple_of(nth * (2 * BLOCK), BLOCK)
                box[dst // NX, : 2 * BLOCK, :] = got[sx, pl.ds(at, 2 * BLOCK), :]

        return carry

    lax.fori_loop(0, move_count(moves), body, 0)


def pick_arrival(pos, moves, got, box, total):
    me = pos[0] * NX + pos[1]
    tally = got[0, 2 * BLOCK : 2 * BLOCK + 8, :].astype(jnp.float32)
    for i in range(1, NY):
        tally = tally + got[i, 2 * BLOCK : 2 * BLOCK + 8, :].astype(jnp.float32)
    total[...] = jnp.broadcast_to(jnp.sum(tally, axis=1, keepdims=True), total.shape)

    def came(m, at):
        return jnp.where(moves[1, m] == me, moves[0, m] // NX, at)

    sy = lax.fori_loop(0, move_count(moves), came, 0)
    for d in range(NZ):
        box[d] = got[sy, : 2 * BLOCK, :]


def compute(
    pos, moves, total, mine, other, late, late_other, wg, wu, wd,
    hidden, by_x, by_y, tok, grad, hid, back,
):
    j = pl.program_id(0)
    span = WORK * BLOCK
    tile = wg.shape[1]
    width = hid.shape[1]
    steps = width // tile

    @pl.when(j == 0)
    def _():
        me = pos[0] * NX + pos[1]
        first = pos[3] == 0
        for z in range(NZ):
            a, b = mine[z], other[z]
            low = jnp.where(first, a, b)
            high = jnp.where(first, b, a)
            at = z * 2 * BLOCK
            tok[:, at : at + BLOCK] = low[:span]
            grad[:, at : at + BLOCK] = low[span:]
            tok[:, at + BLOCK : at + 2 * BLOCK] = high[:span]
            grad[:, at + BLOCK : at + 2 * BLOCK] = high[span:]

        def own(b, nth):
            def gone(m, hit):
                return hit | ((moves[0, m] == me) & (moves[2, m] == b)).astype(jnp.int32)

            left = lax.fori_loop(0, move_count(moves), gone, 0)
            return nth + ((b * BLOCK < pos[2]) & (left == 0)).astype(jnp.int32)

        def came(m, hit):
            return hit | (moves[1, m] == me).astype(jnp.int32)

        nth = lax.fori_loop(0, CAP, own, 0)
        here = lax.fori_loop(0, move_count(moves), came, 0)

        @pl.when((here == 1) & (nth < WORK))
        def _():
            rows = pl.ds(pl.multiple_of(nth * BLOCK, BLOCK), BLOCK)
            for z in range(NZ):
                a, b = late[z], late_other[z]
                low = jnp.where(first, a, b)
                high = jnp.where(first, b, a)
                at = z * 2 * BLOCK
                tok[rows, at : at + BLOCK] = low[:BLOCK]
                grad[rows, at : at + BLOCK] = low[BLOCK:]
                tok[rows, at + BLOCK : at + 2 * BLOCK] = high[:BLOCK]
                grad[rows, at + BLOCK : at + 2 * BLOCK] = high[BLOCK:]

    for i in range(steps):

        @pl.when(j == i)
        def _():
            gate_sum = jnp.dot(tok[...], wg[...], preferred_element_type=jnp.float32)
            up_sum = jnp.dot(tok[...], wu[...], preferred_element_type=jnp.float32)
            back_sum = jnp.dot(grad[...], wd[...], preferred_element_type=jnp.float32)
            logistic = jax.nn.sigmoid(gate_sum)
            act = gate_sum * logistic
            value = (act * up_sum).astype(jnp.bfloat16)
            hidden[...] = value
            at = i * tile
            hid[:, at : at + tile] = value
            back[:, at : at + tile] = (
                back_sum * up_sum * logistic * (1.0 + gate_sum * (1.0 - logistic))
            ).astype(jnp.bfloat16)
            back[:, width + at : width + at + tile] = (back_sum * act).astype(jnp.bfloat16)

    for i in range(NY):

        @pl.when(j == steps + i)
        def _():
            inv = 1.0 / total[0, 0]
            per = by_x.shape[2]
            at = i * NX * per

            def term(left, right):
                out = lax.dot_general(
                    left, right, (((0,), (0,)), ((), ())), preferred_element_type=jnp.float32
                )
                return (out * inv).astype(jnp.bfloat16)

            both = term(tok[:, at : at + NX * per], back[...])
            for x in range(NX):
                by_x[x, 0] = both[x * per : (x + 1) * per, width:]
            by_y[0, :, :width] = both[:, :width]
            by_y[0, :, width:] = term(grad[:, at : at + NX * per], hid[...])


def add_x(got, out):
    acc = got[0].astype(jnp.float32)
    for i in range(1, NX):
        acc = acc + got[i].astype(jnp.float32)
    out[...] = acc.astype(jnp.bfloat16)


def finish(from_y, from_x, gate, up, down):
    acc = from_y[0].astype(jnp.float32)
    for i in range(1, NY):
        acc = acc + from_y[i].astype(jnp.float32)
    up[...] = acc
    bcc = from_x[0].astype(jnp.float32)
    for i in range(1, NX):
        bcc = bcc + from_x[i].astype(jnp.float32)
    width = gate.shape[1]
    gate[...] = bcc[:, :width]
    down[...] = bcc[:, width:]


def a2a(value, axis):
    return lax.all_to_all(value, axis, split_axis=0, concat_axis=0, tiled=True)


def swap(value):
    return lax.ppermute(value, "c", [(0, 1), (1, 0)])


def on_device(
    tokens, out_grad, counts, block_moves, segment_ids, gate_weight, up_weight, down_weight
):
    bf = jnp.bfloat16
    f32 = jnp.float32
    slots, feat = tokens.shape
    per, hid = gate_weight.shape
    span = WORK * BLOCK
    model = 2 * NZ * feat
    weights = lax.all_gather(
        jnp.concatenate([gate_weight, up_weight, down_weight], axis=1), ROW, axis=0, tiled=True
    )
    pos = jnp.stack([lax.axis_index("y"), lax.axis_index("x"), counts[0], lax.axis_index("c")])
    moves = block_moves.T
    box, work = pl.pallas_call(
        pack_x,
        out_shape=(
            jax.ShapeDtypeStruct((NX, 4 * BLOCK + NTAG, feat), bf),
            jax.ShapeDtypeStruct((NZ, 2 * span, feat), bf),
        ),
        in_specs=[smem(), smem(), vmem(), vmem(), vmem()],
        out_specs=(vmem(), vmem()),
        scratch_shapes=[pltpu.VMEM((slots, feat), bf)],
        compiler_params=params(),
        name="pack_x",
    )(pos, moves, segment_ids.reshape(CAP, BLOCK), tokens, out_grad)
    mine = a2a(work, "z")
    got = a2a(box, "x")
    box = pl.pallas_call(
        pack_y,
        out_shape=jax.ShapeDtypeStruct((NY, 2 * BLOCK + NTAG, feat), bf),
        in_specs=[smem(), smem(), vmem()],
        out_specs=vmem(),
        scratch_shapes=[pltpu.SMEM((NX,), jnp.int32)],
        compiler_params=params(),
        name="pack_y",
    )(pos, moves, got)
    got = a2a(box, "y")
    box, total = pl.pallas_call(
        pick_arrival,
        out_shape=(
            jax.ShapeDtypeStruct((NZ, 2 * BLOCK, feat), bf),
            jax.ShapeDtypeStruct((8, BLOCK), f32),
        ),
        in_specs=[smem(), smem(), vmem()],
        out_specs=(vmem(), vmem()),
        compiler_params=params(),
        name="pick_arrival",
    )(pos, moves, got)
    late = a2a(box, "z")
    other = swap(mine)
    late_other = swap(late)

    tile = 256
    steps = hid // tile

    def whole(shape):
        return pl.BlockSpec(shape, lambda j: (0,) * len(shape))

    def cols(rows, offset):
        return pl.BlockSpec((rows, tile), lambda j: (0, jnp.minimum(j, steps - 1) + offset))

    def later(j):
        return jnp.maximum(j - steps, 0)

    hidden, by_x, by_y = pl.pallas_call(
        compute,
        grid=(steps + NY,),
        out_shape=(
            jax.ShapeDtypeStruct((span, hid), bf),
            jax.ShapeDtypeStruct((NX, NY, per, hid), bf),
            jax.ShapeDtypeStruct((NY, NX * per, 2 * hid), bf),
        ),
        in_specs=[
            smem(),
            smem(),
            whole((8, BLOCK)),
            whole((NZ, 2 * span, feat)),
            whole((NZ, 2 * span, feat)),
            whole((NZ, 2 * BLOCK, feat)),
            whole((NZ, 2 * BLOCK, feat)),
            cols(model, 0),
            cols(model, steps),
            cols(model, 2 * steps),
        ],
        out_specs=(
            cols(span, 0),
            pl.BlockSpec((NX, 1, per, hid), lambda j: (0, later(j), 0, 0)),
            pl.BlockSpec((1, NX * per, 2 * hid), lambda j: (later(j), 0, 0)),
        ),
        scratch_shapes=[
            pltpu.VMEM((span, model), bf),
            pltpu.VMEM((span, model), bf),
            pltpu.VMEM((span, hid), bf),
            pltpu.VMEM((span, 2 * hid), bf),
        ],
        compiler_params=params(dimension_semantics=("arbitrary",)),
        name="compute",
    )(pos, moves, total, mine, other, late, late_other, weights, weights, weights)

    part_y = lax.psum_scatter(
        by_y.reshape(NY * NX * per, 2 * hid), "y", scatter_dimension=0, tiled=True
    )
    part_x = pl.pallas_call(
        add_x,
        out_shape=jax.ShapeDtypeStruct((NY, per, hid), bf),
        in_specs=[vmem()],
        out_specs=vmem(),
        compiler_params=params(),
        name="add_x",
    )(a2a(by_x, "x"))
    from_y = a2a(part_x, "y")
    from_x = a2a(part_y.reshape(NX, per, 2 * hid), "x")
    gate_grad, up_grad, down_grad = pl.pallas_call(
        finish,
        out_shape=tuple(jax.ShapeDtypeStruct((per, hid), f32) for _ in range(3)),
        in_specs=[vmem(), vmem()],
        out_specs=(vmem(), vmem(), vmem()),
        compiler_params=params(),
        name="finish",
    )(from_y, from_x)
    return (hidden, gate_grad, up_grad, down_grad)


def solution(mesh):
    torus = Mesh(mesh.devices.reshape(NY, NX, NZ, 2), ("y", "x", "z", "c"))
    return jax.shard_map(
        on_device,
        mesh=torus,
        in_specs=(P(ROW, COL), P(ROW, COL), P(ROW), P(), P(ROW), P(ROW, COL), P(ROW, COL), P(ROW, COL)),
        out_specs=(P(ROW, COL), P(ROW, COL), P(ROW, COL), P(ROW, COL)),
        check_vma=False,
    )
```

time: 244 us -> 248 us (1.016)
  the two profiles are of different devices: /device:TPU:2 before, /device:TPU:64 now
where the time goes in v2:
time: 248 us; the launch traced here: 247 us
  blocking collectives  108 us (44%)
  waiting for transfers between devices  68.5 us (28%)
  Pallas kernels  30 us (12%)
  starting transfers between devices  21 us (8%)
  between operations  14.7 us (6%)
  local copies, waits for them, and re-layouts  3.16 us (1%)
    all_to_all x5, blocking collectives, a2a(): return lax.all_to_all(value, axis, split_axis=0, concat_axis=0, tiled=True)  108 us
    all_to_all x2, waiting for transfers between devices, a2a(): return lax.all_to_all(value, axis, split_axis=0, concat_axis=0, tiled=True)  66.5 us
    all_to_all x2, starting transfers between devices, a2a(): return lax.all_to_all(value, axis, split_axis=0, concat_axis=0, tiled=True)  17.1 us
    pallas_call x1, Pallas kernels, on_device(): pl.pallas_call(compute, grid=(steps + NY,), out_shape=(jax.ShapeDtypeStru...  16.8 us
  transfers between devices with their start and end apart: 6, of which 3 were waited for; matrix products, arithmetic and copies ran while one was open for 0% of the time, Pallas kernels for 5%

profile of v2, /device:TPU:64, one launch (start us, length us, event | category | flops | bytes accessed | tf_op | source)
XLA Modules:
  0.0 247.2 jit_solution(14296608326609893684)
XLA Ops:
  7.2 0.0 all-gather.2.cloned.1.call-start
  7.2 1.6 pad_maximum_fusion
  8.8 0.0 all-gather.2.cloned.1.call-update
  9.5 0.7 pad_add_fusion.pos
  10.1 4.2 %pack_x.1 = (bf16[4,528,128]{2,1,0:T(8,128)(2,1)}, bf16[8,1024,128]{2,1,0:T(8,128)(2,1)}) custom-call(s32[4]{0:T(128)} %pad_add_fusion.pos, s32[3,16]{1,0:T(4,128)} %bitcast.9, s32[6,128]{1,0:T(8,128)} %bitcast.13, bf16[768,128]{1,0:T(8,128)(2,1)} %tok.1, bf16[768,128]{1,0:T(8,128)(2,1)} %grad.1), custom_call_target="tpu_custom_call" | custom-call | tf_op jit(solution)/shard_map/pack_x/pallas_call | solution.py:265
  14.3 14.1 %all_to_all.35.got = bf16[4,528,128]{2,1,0:T(8,128)(2,1)} all-to-all(bf16[4,528,128]{2,1,0:T(8,128)(2,1)} %get-tuple-element.14), channel_id=1, replica_groups=mesh['y'=8,'x'=4,'z'=8,'c'=2] {'x'}, dimensions={0} | all-to-all | bytes 1081344 | tf_op jit(solution)/shard_map/all_to_all | solution.py:244
  28.5 10.0 %all-to-all-start.2 = ((bf16[8,1024,128]{2,1,0:T(8,128)(2,1)}), bf16[8,1024,128]{2,1,0:T(8,128)(2,1)S(1)}, u32[]{:S(2)}, u32[]{:S(2)}) async-start(bf16[8,1024,128]{2,1,0:T(8,128)(2,1)} %get-tuple-element.16), calls=%async_computation.2 | async-start | bytes 4194304 | tf_op jit(solution)/shard_map/all_to_all | solution.py:244
  38.4 2.3 pack_y.1
  40.7 46.2 %all-to-all-done.2.mine = bf16[8,1024,128]{2,1,0:T(8,128)(2,1)S(1)} async-done(((bf16[8,1024,128]{2,1,0:T(8,128)(2,1)}), bf16[8,1024,128]{2,1,0:T(8,128)(2,1)S(1)}, u32[]{:S(2)}, u32[]{:S(2)}) %all-to-all-start.2) | async-done | bytes 2097184 | tf_op jit(solution)/shard_map/all_to_all | solution.py:244
  86.8 0.0 copy-start
  86.8 7.1 %all-to-all-start.1 = ((bf16[8,272,128]{2,1,0:T(8,128)(2,1)}), bf16[8,272,128]{2,1,0:T(8,128)(2,1)S(1)}, u32[]{:S(2)}, u32[]{:S(2)}) async-start(bf16[8,272,128]{2,1,0:T(8,128)(2,1)} %pack_y.1), calls=%async_computation.1 | async-start | bytes 1114112 | tf_op jit(solution)/shard_map/all_to_all | solution.py:244
  93.9 0.0 reduce-scatter.2.cloned.1.call-start
  94.0 1.9 collective-permute-start
  95.9 20.4 %all-to-all-done.1.got = bf16[8,272,128]{2,1,0:T(8,128)(2,1)S(1)} async-done(((bf16[8,272,128]{2,1,0:T(8,128)(2,1)}), bf16[8,272,128]{2,1,0:T(8,128)(2,1)S(1)}, u32[]{:S(2)}, u32[]{:S(2)}) %all-to-all-start.1) | async-done | bytes 557088 | tf_op jit(solution)/shard_map/all_to_all | solution.py:244
  116.3 0.0 copy-start.1
  116.3 0.8 copy-done.1
  117.1 2.1 pick_arrival.1
  119.2 23.0 %all_to_all.36.late = bf16[8,256,128]{2,1,0:T(8,128)(2,1)S(1)} all-to-all(bf16[8,256,128]{2,1,0:T(8,128)(2,1)} %get-tuple-element.17), channel_id=1, replica_groups=mesh['y'=8,'x'=4,'z'=8,'c'=2] {'z'}, dimensions={0} | all-to-all | bytes 1048576 | tf_op jit(solution)/shard_map/all_to_all | solution.py:244
  142.2 1.9 collective-permute-start.1
  144.1 1.9 collective-permute-done.1.late_other
  146.0 0.0 collective-permute-done.other
  146.0 0.0 copy-done
  146.0 0.0 copy-done.2
  146.0 0.8 copy-done.4
  146.8 16.8 %compute.1 = (bf16[512,512]{1,0:T(8,128)(2,1)}, bf16[4,8,64,512]{3,2,1,0:T(8,128)(2,1)}, bf16[8,256,1024]{2,1,0:T(8,128)(2,1)}) custom-call(s32[4]{0:T(128)} %pad_add_fusion.pos, s32[3,16]{1,0:T(4,128)} %bitcast.12, f32[8,128]{1,0:T(8,128)} %get-tuple-element.15.total, bf16[8,1024,128]{2,1,0:T(8,128)(2,1)} %copy-done, ...), custom_call_target="tpu_custom_call" | custom-call | tf_op jit(solution)/shard_map/compute/pallas_call | solution.py:316
  163.6 0.0 reduce-scatter.2.cloned.1.call-update
  163.6 1.6 copy-done.3
  165.2 30.1 %all_to_all.37.got = bf16[4,8,64,512]{3,2,1,0:T(8,128)(2,1)} all-to-all(bf16[4,8,64,512]{3,2,1,0:T(8,128)(2,1)S(1)} %copy-done.3), channel_id=1, replica_groups=mesh['y'=8,'x'=4,'z'=8,'c'=2] {'x'}, dimensions={0} | all-to-all | bytes 4194304 | tf_op jit(solution)/shard_map/all_to_all | solution.py:244
  195.3 2.7 %add_x.1 = bf16[8,64,512]{2,1,0:T(8,128)(2,1)} custom-call(bf16[4,8,64,512]{3,2,1,0:T(8,128)(2,1)} %all_to_all.37.got), custom_call_target="tpu_custom_call" | custom-call | tf_op jit(solution)/shard_map/add_x/pallas_call | solution.py:354
  198.0 26.9 %all_to_all.38.from_y = bf16[8,64,512]{2,1,0:T(8,128)(2,1)} all-to-all(bf16[8,64,512]{2,1,0:T(8,128)(2,1)} %add_x.1), channel_id=1, replica_groups=mesh['y'=8,'x'=4,'z'=8,'c'=2] {'y'}, dimensions={0} | all-to-all | bytes 1048576 | tf_op jit(solution)/shard_map/all_to_all | solution.py:244
  224.9 13.4 %all_to_all.39.from_x = bf16[4,64,1024]{2,1,0:T(8,128)(2,1)} all-to-all(bf16[4,64,1024]{2,1,0:T(8,128)(2,1)} %bitcast.8), channel_id=1, replica_groups=mesh['y'=8,'x'=4,'z'=8,'c'=2] {'x'}, dimensions={0} | all-to-all | bytes 1048576 | tf_op jit(solution)/shard_map/all_to_all | solution.py:244
  238.3 2.0 finish.1
  (5 shorter events, 0.0 us)
Async XLA Ops:
  7.2 138.9 %all-gather.2.cloned.1.call-start = ((), (), s32[]{:S(2)}) async-start(), calls=%async_computation.8 | async-start | bytes 6488064 | tf_op jit(solution)/shard_map/all_gather | solution.py:260
  28.5 58.4 %all-to-all-start.2 = ((bf16[8,1024,128]{2,1,0:T(8,128)(2,1)}), bf16[8,1024,128]{2,1,0:T(8,128)(2,1)S(1)}, u32[]{:S(2)}, u32[]{:S(2)}) async-start(bf16[8,1024,128]{2,1,0:T(8,128)(2,1)} %get-tuple-element.16), calls=%async_computation.2 | async-start | bytes 4194304 | tf_op jit(solution)/shard_map/all_to_all | solution.py:244
  86.8 59.2 %copy-start = (bf16[8,1024,128]{2,1,0:T(8,128)(2,1)}, bf16[8,1024,128]{2,1,0:T(8,128)(2,1)S(1)}, u32[]{:S(2)}) copy-start(bf16[8,1024,128]{2,1,0:T(8,128)(2,1)S(1)} %all-to-all-done.2.mine) | copy-start | bytes 6291460
  86.8 29.5 %all-to-all-start.1 = ((bf16[8,272,128]{2,1,0:T(8,128)(2,1)}), bf16[8,272,128]{2,1,0:T(8,128)(2,1)S(1)}, u32[]{:S(2)}, u32[]{:S(2)}) async-start(bf16[8,272,128]{2,1,0:T(8,128)(2,1)} %pack_y.1), calls=%async_computation.1 | async-start | bytes 1114112 | tf_op jit(solution)/shard_map/all_to_all | solution.py:244
  93.9 131.0 %reduce-scatter.2.cloned.1.call-start = ((), (), s32[]{:S(2)}) async-start(), calls=%async_computation.9 | async-start | bytes 4718592 | tf_op jit(solution)/shard_map/reduce_scatter | solution.py:351
  94.0 52.1 %collective-permute-start = (bf16[8,1024,128]{2,1,0:T(8,128)(2,1)S(1)}, bf16[8,1024,128]{2,1,0:T(8,128)(2,1)}, u32[]{:S(2)}, u32[]{:S(2)}) collective-permute-start(bf16[8,1024,128]{2,1,0:T(8,128)(2,1)S(1)} %all-to-all-done.2.mine), channel_id=1, source_target_pairs={{0,1},{1,0},{2,3},{3,2},{4,5},{5,4},{6,7},{7,6},{8,9},{9,8},{10,11... | collective-permute-start | bytes 6291464 | tf_op jit(solution)/shard_map/ppermute | solution.py:248
  116.3 0.8 copy-start.1
  142.2 3.8 %copy-start.2 = (bf16[8,256,128]{2,1,0:T(8,128)(2,1)}, bf16[8,256,128]{2,1,0:T(8,128)(2,1)S(1)}, u32[]{:S(2)}) copy-start(bf16[8,256,128]{2,1,0:T(8,128)(2,1)S(1)} %all_to_all.36.late) | copy-start | bytes 1572868
  142.2 3.8 %collective-permute-start.1 = (bf16[8,256,128]{2,1,0:T(8,128)(2,1)S(1)}, bf16[8,256,128]{2,1,0:T(8,128)(2,1)S(1)}, u32[]{:S(2)}, u32[]{:S(2)}) collective-permute-start(bf16[8,256,128]{2,1,0:T(8,128)(2,1)S(1)} %all_to_all.36.late), channel_id=1, source_target_pairs={{0,1},{1,0},{2,3},{3,2},{4,5},{5,4},{6,7},{7,6},{8,9},{9,8},{10,11... | collective-permute-start | bytes 1572872 | tf_op jit(solution)/shard_map/ppermute | solution.py:248
  146.0 0.8 copy-start.4
  163.6 1.6 copy-start.3
Sparse Core Ops, SparseCore 0:
  11.1 108.6 all-gather.1
  163.7 58.1 reduce-scatter.1
